TPU v7x, 16 devices: a 4x2x1 block of a 4x4x8 slice. The times are simulated.
16 devices in a mesh: rep: 4 (over y, z, core), dp: 4 (over x).
Axes of the slice: x: 4, y: 2, z: 1, core: 2. Of those that a mesh axis runs over, the one named last changes fastest.
The devices are a block of a 4x4x8 slice.
Arguments:
- a: bfloat16 [16, 4, 4096, 768], P(('rep', 'dp')), parts along dimension 0
- g: bfloat16 [16, 4, 4096, 3072], P(('rep', 'dp')), parts along dimension 0
Outputs:
- output: bfloat16 [16, 768, 3072], P('rep'), parts along dimension 0
There are 4 independent parts. A program takes and returns all parts, laid end to end along the dimension named above; each array names one.
All inputs are finite; a program needn't handle non-finite values.
Results may differ from a plain program's by a relative error of at most 0.012.
Values are sent between devices in bfloat16 or wider.
A program may use at most 768 MiB of HBM per device.

v0:
```python
import jax
import jax.numpy as jnp


def solution(mesh):
    groups = mesh.shape["rep"]

    def step(a, g):
        a, g = (t.reshape(groups, -1, *t.shape[1:]) for t in (a, g))
        sums = jnp.einsum("rsntd,rsntf->rndf", a, g, preferred_element_type=jnp.float32)
        return sums.astype(jnp.bfloat16).reshape(-1, *sums.shape[2:])

    return step
```

profile of v0, /device:TPU:112, one launch (start us, length us, event | category | flops | bytes accessed | tf_op | source)
XLA Modules:
  0.0 728.4 jit_solution(14337711546172939803)
XLA Ops:
  0.0 88.8 %fusion.3 = f32[1,4,768,3072]{3,2,1,0:T(8,128)} fusion(bf16[1,4,4096,3072]{3,2,1,0:T(8,128)(2,1)} %param.1, bf16[1,4,4096,768]{3,2,1,0:T(8,128)(2,1)} %param), kind=kOutput, calls=%fused_computation.4 | convolution fusion | flops 77309411328 | bytes 163577856 | tf_op jit(solution)/rsntd,rsntf->rndf/dot_general | solution.py:10
  88.8 639.6 %all-reduce.2 = bf16[1,4,768,3072]{3,2,1,0:T(8,128)(2,1)} all-reduce(f32[1,4,768,3072]{3,2,1,0:T(8,128)} %fusion.3), channel_id=1, replica_groups=[4,4]<=[16], use_global_device_ids=true, to_apply=%add.clone | all-reduce | flops 9437184 | bytes 56623104 | tf_op jit(solution)/rsntd,rsntf->rndf/dot_general | solution.py:10
where the time goes:
time: 728 us
  blocking collectives  640 us (88%)
  matrix products  88.8 us (12%)
    dot_general x1, blocking collectives, step(): jnp.einsum('rsntd,rsntf->rndf', a, g, preferred_element_type=jnp.float32)  640 us
    dot_general x1, matrix products, step(): jnp.einsum('rsntd,rsntf->rndf', a, g, preferred_element_type=jnp.float32)  88.8 us

commit v1 on v0

v1 whole, which is shorter than its diff:
```python
import functools

import jax
import jax.numpy as jnp
from jax import lax
from jax.experimental import pallas as pl
from jax.experimental.pallas import tpu as pltpu
from jax.sharding import PartitionSpec as P

COLS = 256
ROWS = 256
SLOTS = 3


def ring_kernel(ranks, a_hbm, g_hbm, sums, a_v, g_v, a_sem, g_sem, send_sem, recv_sem):
    mats, blocks, rows, _ = sums.shape
    per_mat = blocks // ranks
    units = mats * per_mat
    me = lax.axis_index("dp")
    right = lax.rem(me + 1, ranks)
    left = lax.rem(me + ranks - 1, ranks)

    def place(s, w):
        to_left = lax.rem(w, 2)
        b = lax.rem(me + (2 * ranks - s) + to_left * (2 * s), ranks)
        return w // per_mat, lax.rem(w, per_mat) * ranks + b

    def load_a(n):
        return pltpu.make_async_copy(a_hbm.at[0, n], a_v.at[n], a_sem.at[n])

    def load_g(i):
        n, c = place(i // units, lax.rem(i, units))
        slot = lax.rem(i, SLOTS)
        columns = pl.ds(pl.multiple_of(c * COLS, COLS), COLS)
        return pltpu.make_async_copy(g_hbm.at[0, n, :, columns], g_v.at[slot], g_sem.at[slot])

    def send(s, w, part):
        n, c = place(s, w)
        block = sums.at[n, c] if part is None else sums.at[n, c, part]
        to = right + lax.rem(w, 2) * (left - right)
        return pltpu.make_async_remote_copy(
            src_ref=block,
            dst_ref=block,
            send_sem=send_sem.at[s, w],
            recv_sem=recv_sem.at[s, w],
            device_id={"dp": to},
            device_id_type=pl.DeviceIdType.MESH,
        )

    def arrived(s, w):
        n, c = place(s + 1, w)
        pltpu.make_async_copy(sums.at[n, c], sums.at[n, c], recv_sem.at[s, w]).wait()

    def free(i):
        old = i - (ranks - 2) * units + 1

        @pl.when(jnp.logical_and(old >= 0, old < (ranks - 1) * units))
        def _():
            send(old // units, lax.rem(old, units), None).wait_send()

    load_a(0).start()
    load_g(0).start()
    load_g(1).start()
    for n in range(1, mats):
        load_a(n).start()

    barrier = pltpu.get_barrier_semaphore()
    for neighbour in (left, right):
        pl.semaphore_signal(barrier, inc=1, device_id={"dp": neighbour}, device_id_type=pl.DeviceIdType.MESH)
    pl.semaphore_wait(barrier, 2)

    def item(i, first):
        s, w = i // units, lax.rem(i, units)
        n, c = place(s, w)

        @pl.when(i + 2 < ranks * units)
        def _():
            load_g(i + 2).start()

        if first:

            @pl.when(lax.rem(w, per_mat) == 0)
            def _():
                load_a(n).wait()

        load_g(i).wait()
        if not first:
            arrived(s - 1, w)
            free(i)
        slot = lax.rem(i, SLOTS)
        for m in range(0, rows, ROWS):
            part = pl.ds(m, ROWS)
            term = lax.dot_general(
                a_v[n, :, m : m + ROWS],
                g_v[slot],
                (((0,), (0,)), ((), ())),
                preferred_element_type=jnp.float32,
            )
            if not first:
                term += sums[n, c, part].astype(jnp.float32)
            sums[n, c, part] = term.astype(sums.dtype)
            send(s, w, part).start()

    def first_item(i, carry):
        item(i, True)
        return carry

    def later_item(i, carry):
        item(i, False)
        return carry

    def forward(j, carry):
        s, w = j // units, lax.rem(j, units)
        arrived(s - 1, w)
        free(j)
        send(s, w, None).start()
        return carry

    def finish(j, carry):
        s, w = j // units, lax.rem(j, units)
        send(s, w, None).wait_send()
        return carry

    def last(w, carry):
        arrived(2 * ranks - 3, w)
        return carry

    lax.fori_loop(0, units, first_item, 0)
    lax.fori_loop(units, ranks * units, later_item, 0)
    lax.fori_loop(ranks * units, (2 * ranks - 2) * units, forward, 0)
    lax.fori_loop(0, units, last, 0)
    lax.fori_loop((ranks - 1) * units, (2 * ranks - 2) * units, finish, 0)


def write_kernel(sums, out, sem):
    mats, blocks = sums.shape[:2]

    def copy(n, c):
        return pltpu.make_async_copy(sums.at[n, c], out.at[n, :, pl.ds(c * COLS, COLS)], sem.at[n, c])

    for n in range(mats):
        for c in range(blocks):
            copy(n, c).start()
    for n in range(mats):
        for c in range(blocks):
            copy(n, c).wait()


def solution(mesh):
    ranks = mesh.shape["dp"]

    def local(a, g):
        _, mats, tokens, rows = a.shape
        width = g.shape[-1]
        blocks = width // COLS
        units = blocks // ranks * mats
        phases = 2 * ranks - 2
        sums = pl.pallas_call(
            functools.partial(ring_kernel, ranks),
            out_shape=pltpu.VMEM((mats, blocks, rows, COLS), jnp.bfloat16),
            in_specs=[pl.BlockSpec(memory_space=pltpu.HBM)] * 2,
            out_specs=pl.BlockSpec(memory_space=pltpu.VMEM),
            scratch_shapes=[
                pltpu.VMEM((mats, tokens, rows), jnp.bfloat16),
                pltpu.VMEM((SLOTS, tokens, COLS), jnp.bfloat16),
                pltpu.SemaphoreType.DMA((mats,)),
                pltpu.SemaphoreType.DMA((SLOTS,)),
                pltpu.SemaphoreType.DMA((phases, units)),
                pltpu.SemaphoreType.DMA((phases, units)),
            ],
            compiler_params=pltpu.CompilerParams(
                collective_id=0, has_side_effects=True, vmem_limit_bytes=42 * 2**20
            ),
            name="ring",
        )(a, g)
        return pl.pallas_call(
            write_kernel,
            out_shape=jax.ShapeDtypeStruct((mats, rows, width), jnp.bfloat16),
            in_specs=[pl.BlockSpec(memory_space=pltpu.VMEM)],
            out_specs=pl.BlockSpec(memory_space=pltpu.HBM),
            scratch_shapes=[pltpu.SemaphoreType.DMA((mats, blocks))],
            compiler_params=pltpu.CompilerParams(vmem_limit_bytes=2**20),
            name="write",
        )(pltpu.with_memory_space_constraint(sums, pltpu.VMEM))

    return jax.shard_map(
        local, mesh=mesh, in_specs=P(("rep", "dp")), out_specs=P("rep"), check_vma=False
    )
```

time: 728 us -> 324 us (0.45)
  blocking collectives: 640 us -> 0 us
  Pallas kernels: 0 us -> 324 us
  matrix products: 88.8 us -> 0 us
    dot_general x1 -> x0, blocking collectives: 640 us -> none  [step(): jnp.einsum('rsntd,rsntf->rndf', a, g, preferred_element_type=jnp.float32)]
    pallas_call x0 -> x2, Pallas kernels: none -> 324 us  [the longest x1 318 us: local(): pl.pallas_call(functools.partial(ring_kernel, ranks), out_shape=pltpu.VME...]
    dot_general x1 -> x0, matrix products: 88.8 us -> none  [step(): jnp.einsum('rsntd,rsntf->rndf', a, g, preferred_element_type=jnp.float32)]
where the time goes in v1:
time: 324 us
  Pallas kernels  324 us (100%)
    pallas_call x1, Pallas kernels, local(): pl.pallas_call(functools.partial(ring_kernel, ranks), out_shape=pltpu.VME...  318 us
    pallas_call x1, Pallas kernels, local(): pl.pallas_call(write_kernel, out_shape=jax.ShapeDtypeStruct((mats, rows,...  6.84 us

profile of v1, /device:TPU:112, one launch (start us, length us, event | category | flops | bytes accessed | tf_op | source)
XLA Modules:
  0.0 324.4 jit_solution(18063510020841014031)
XLA Ops:
  0.0 317.6 %ring.1.sums = bf16[4,12,768,256]{3,2,1,0:T(8,128)(2,1)S(1)} custom-call(bf16[1,4,4096,768]{3,2,1,0:T(8,128)(2,1)} %a_hbm.1, bf16[1,4,4096,3072]{3,2,1,0:T(8,128)(2,1)} %g_hbm.1), custom_call_target="tpu_custom_call" | custom-call | tf_op jit(solution)/shard_map/ring/pallas_call | solution.py:158
  317.6 6.8 %write.1 = bf16[4,768,3072]{2,1,0:T(8,128)(2,1)} custom-call(bf16[4,12,768,256]{3,2,1,0:T(8,128)(2,1)S(1)} %ring.1.sums), custom_call_target="tpu_custom_call" | custom-call | tf_op jit(solution)/shard_map/write/pallas_call | solution.py:176

commit v2 on v1

v2 whole, which is shorter than its diff:
```python
import functools

import jax
import jax.numpy as jnp
from jax import lax
from jax.experimental import pallas as pl
from jax.experimental.pallas import tpu as pltpu
from jax.sharding import PartitionSpec as P

COLS = 256
ROWS = 256
FIRST = 128
TAIL, LAST = 8, 2
SLOTS = 4


def place(ranks, per_mat, me, s, w):
    to_left = lax.rem(w, 2)
    b = lax.rem(me + 2 * ranks - s + to_left * (2 * s), ranks)
    return w // per_mat, lax.rem(w, per_mat) * ranks + b


def kept(units):
    return units - TAIL + lax.rem(lax.axis_index("rep"), 2) * (TAIL - LAST)


def greet(ranks):
    me = lax.axis_index("dp")
    right = lax.rem(me + 1, ranks)
    left = lax.rem(me + ranks - 1, ranks)
    barrier = pltpu.get_barrier_semaphore()
    for neighbour in (left, right):
        pl.semaphore_signal(barrier, inc=1, device_id={"dp": neighbour}, device_id_type=pl.DeviceIdType.MESH)
    pl.semaphore_wait(barrier, 2)


def ring_kernel(ranks, a_hbm, g_hbm, sums, a_v, g_v, a_sem, a0_sem, g_sem, start_sem, send_sem, recv_sem):
    mats, blocks, rows, _ = sums.shape
    per_mat = blocks // ranks
    units = mats * per_mat
    me = lax.axis_index("dp")
    right = lax.rem(me + 1, ranks)
    left = lax.rem(me + ranks - 1, ranks)

    end = (2 * ranks - 3) * units + kept(units)

    def place_of(s, w):
        return place(ranks, per_mat, me, s, w)

    def load_a(n):
        return pltpu.make_async_copy(a_hbm.at[0, n], a_v.at[n], a_sem.at[n])

    cuts = [0, FIRST, *range(ROWS, rows + 1, ROWS)]
    tokens = a_v.shape[1]

    def load_a0(k):
        columns = pl.ds(cuts[k], cuts[k + 1] - cuts[k])
        return pltpu.make_async_copy(a_hbm.at[0, 0, :, columns], a_v.at[0, :, columns], a0_sem.at[k])

    def load_start(h):
        half = pl.ds(h * (tokens // 2), tokens // 2)
        copies = [(a_hbm.at[0, 0, half, pl.ds(0, FIRST)], a_v.at[0, half, pl.ds(0, FIRST)])]
        for i in range(2):
            n, c = place_of(0, i)
            columns = pl.ds(pl.multiple_of(c * COLS, COLS), COLS)
            copies.append((g_hbm.at[0, n, half, columns], g_v.at[half, pl.ds(i * COLS, COLS)]))
        return [pltpu.make_async_copy(*copy, start_sem.at[h, k]) for k, copy in enumerate(copies)]

    def slot(i):
        return pl.ds(pl.multiple_of(lax.rem(i, SLOTS) * COLS, COLS), COLS)

    def load_g(i):
        n, c = place_of(i // units, lax.rem(i, units))
        columns = pl.ds(pl.multiple_of(c * COLS, COLS), COLS)
        return pltpu.make_async_copy(g_hbm.at[0, n, :, columns], g_v.at[:, slot(i)], g_sem.at[lax.rem(i, SLOTS)])

    def send(s, w, part=()):
        n, c = place_of(s, w)
        block = sums.at[(n, c, *part)]
        to = right + lax.rem(w, 2) * (left - right)
        return pltpu.make_async_remote_copy(
            src_ref=block,
            dst_ref=block,
            send_sem=send_sem.at[s, w],
            recv_sem=recv_sem.at[s, w],
            device_id={"dp": to},
            device_id_type=pl.DeviceIdType.MESH,
        )

    def arrived(s, w):
        n, c = place_of(s + 1, w)
        pltpu.make_async_copy(sums.at[n, c], sums.at[n, c], recv_sem.at[s, w]).wait()

    def free(i):
        old = i - (ranks - 2) * units + 1

        @pl.when(jnp.logical_and(old >= 0, old < (ranks - 1) * units))
        def _():
            send(old // units, lax.rem(old, units)).wait_send()

    for h in range(2):
        for copy in load_start(h):
            copy.start()

    greet(ranks)

    def term_of(n, half, top, bottom, columns):
        return lax.dot_general(
            a_v[n, half, top:bottom],
            g_v[half, columns],
            (((0,), (0,)), ((), ())),
            preferred_element_type=jnp.float32,
        )

    both = slice(0, 2 * COLS)
    for k in range(len(cuts) - 1):
        part = pl.ds(cuts[k], cuts[k + 1] - cuts[k])
        if k == 0:
            term = 0.0
            for h in range(2):
                for copy in load_start(h):
                    copy.wait()
                if h == 0:
                    for later in range(1, len(cuts) - 1):
                        load_a0(later).start()
                    load_g(2).start()
                term += term_of(0, pl.ds(h * (tokens // 2), tokens // 2), 0, FIRST, both)
        else:
            load_a0(k).wait()
            term = term_of(0, slice(None), cuts[k], cuts[k + 1], both)
        for i in range(2):
            n, c = place_of(0, i)
            sums[n, c, part] = term[:, i * COLS : (i + 1) * COLS].astype(sums.dtype)
            send(0, i, (part,)).start()
        if k == 0:
            load_a(1).start()
            load_g(3).start()
    load_g(4).start()
    load_g(5).start()

    def item(i, first):
        s, w = i // units, lax.rem(i, units)
        n = w // per_mat

        if first:

            @pl.when(lax.rem(w, per_mat) == 0)
            def _():
                load_a(n).wait()

            @pl.when(jnp.logical_and(lax.rem(w, per_mat) == 0, n + 1 < mats))
            def _():
                load_a(n + 1).start()

        load_g(i).wait()
        if not first:
            arrived(s - 1, w)
            free(i)
        n, c = place_of(s, w)
        for top in range(0, rows, ROWS):
            part = pl.ds(top, ROWS)
            term = term_of(n, slice(None), top, top + ROWS, slot(i))
            if not first:
                term += sums[n, c, part].astype(jnp.float32)
            sums[n, c, part] = term.astype(sums.dtype)
            send(s, w, (part,)).start()

        @pl.when(i + SLOTS < ranks * units)
        def _():
            load_g(i + SLOTS).start()

    def first_item(i, carry):
        item(i, True)
        return carry

    def later_item(i, carry):
        item(i, False)
        return carry

    def forward(j, carry):
        s, w = j // units, lax.rem(j, units)
        arrived(s - 1, w)
        free(j)
        send(s, w).start()
        return carry

    def finish(j, carry):
        s, w = j // units, lax.rem(j, units)
        send(s, w).wait_send()
        return carry

    def last(j, carry):
        arrived(j // units, lax.rem(j, units))
        return carry

    lax.fori_loop(2, units, first_item, 0)
    lax.fori_loop(units, ranks * units, later_item, 0)
    lax.fori_loop(ranks * units, end, forward, 0)
    lax.fori_loop(end - units, end, last, 0)
    lax.fori_loop((ranks - 1) * units, end, finish, 0)


def tail_kernel(ranks, sums, written, tail, send_sem, recv_sem):
    del written
    mats, blocks = sums.shape[:2]
    per_mat = blocks // ranks
    units = mats * per_mat
    me = lax.axis_index("dp")
    right = lax.rem(me + 1, ranks)
    left = lax.rem(me + ranks - 1, ranks)

    def send(w):
        n, c = place(ranks, per_mat, me, 2 * ranks - 3, w)
        t = w - (units - TAIL)
        return pltpu.make_async_remote_copy(
            src_ref=sums.at[n, c],
            dst_ref=tail.at[t],
            send_sem=send_sem.at[t],
            recv_sem=recv_sem.at[t],
            device_id={"dp": right + lax.rem(w, 2) * (left - right)},
            device_id_type=pl.DeviceIdType.MESH,
        )

    def start(w, carry):
        send(w).start()
        return carry

    def finish(w, carry):
        send(w).wait()
        return carry

    greet(ranks)
    lax.fori_loop(kept(units), units, start, 0)
    lax.fori_loop(kept(units), units, finish, 0)


def write_kernel(ranks, sums, out, sem):
    mats, blocks = sums.shape[:2]
    per_mat = blocks // ranks
    units = mats * per_mat
    me = lax.axis_index("dp")

    def copies(act):
        for w in range(units):
            for s in range(ranks):
                n, c = place(ranks, per_mat, me, s, w)
                columns = pl.ds(pl.multiple_of(c * COLS, COLS), COLS)
                copy = pltpu.make_async_copy(sums.at[n, c], out.at[n, :, columns], sem.at[w, s])
                if s == ranks - 2 and w >= units - TAIL:
                    pl.when(w < kept(units))(functools.partial(act, copy))
                else:
                    act(copy)

    copies(lambda copy: copy.start())
    copies(lambda copy: copy.wait())


def rest_kernel(ranks, per_mat, units, written, tail, out, sem):
    del written
    me = lax.axis_index("dp")

    def copies(act):
        for t in range(TAIL):
            w = units - TAIL + t
            n, c = place(ranks, per_mat, me, ranks - 2, w)
            columns = pl.ds(pl.multiple_of(c * COLS, COLS), COLS)
            copy = pltpu.make_async_copy(tail.at[t], out.at[n, :, columns], sem.at[t])
            pl.when(w >= kept(units))(functools.partial(act, copy))

    copies(lambda copy: copy.start())
    copies(lambda copy: copy.wait())


def solution(mesh):
    ranks = mesh.shape["dp"]

    def local(a, g):
        _, mats, tokens, rows = a.shape
        width = g.shape[-1]
        blocks = width // COLS
        units = blocks // ranks * mats
        phases = 2 * ranks - 2
        sums = pl.pallas_call(
            functools.partial(ring_kernel, ranks),
            out_shape=pltpu.VMEM((mats, blocks, rows, COLS), jnp.bfloat16),
            in_specs=[pl.BlockSpec(memory_space=pltpu.HBM)] * 2,
            out_specs=pl.BlockSpec(memory_space=pltpu.VMEM),
            scratch_shapes=[
                pltpu.VMEM((mats, tokens, rows), jnp.bfloat16),
                pltpu.VMEM((tokens, SLOTS * COLS), jnp.bfloat16),
                pltpu.SemaphoreType.DMA((mats,)),
                pltpu.SemaphoreType.DMA((1 + rows // ROWS,)),
                pltpu.SemaphoreType.DMA((SLOTS,)),
                pltpu.SemaphoreType.DMA((2, 3)),
                pltpu.SemaphoreType.DMA((phases, units)),
                pltpu.SemaphoreType.DMA((phases, units)),
            ],
            compiler_params=pltpu.CompilerParams(
                collective_id=0, has_side_effects=True, vmem_limit_bytes=44 * 2**20
            ),
            name="ring",
        )(a, g)
        sums = pltpu.with_memory_space_constraint(sums, pltpu.VMEM)
        hbm, vmem = pl.BlockSpec(memory_space=pltpu.HBM), pl.BlockSpec(memory_space=pltpu.VMEM)
        whole = jax.ShapeDtypeStruct((mats, rows, width), jnp.bfloat16)
        written = pl.pallas_call(
            functools.partial(write_kernel, ranks),
            out_shape=whole,
            in_specs=[vmem],
            out_specs=hbm,
            scratch_shapes=[pltpu.SemaphoreType.DMA((units, ranks))],
            compiler_params=pltpu.CompilerParams(vmem_limit_bytes=2**20),
            name="write",
        )(sums)
        tail = pl.pallas_call(
            functools.partial(tail_kernel, ranks),
            out_shape=pltpu.VMEM((TAIL, rows, COLS), jnp.bfloat16),
            in_specs=[vmem, hbm],
            out_specs=vmem,
            scratch_shapes=[pltpu.SemaphoreType.DMA((TAIL,))] * 2,
            compiler_params=pltpu.CompilerParams(
                collective_id=1, has_side_effects=True, vmem_limit_bytes=2**20
            ),
            name="tail",
        )(sums, pltpu.with_memory_space_constraint(written, pltpu.HBM))
        return pl.pallas_call(
            functools.partial(rest_kernel, ranks, blocks // ranks, units),
            out_shape=whole,
            in_specs=[hbm, vmem],
            out_specs=hbm,
            input_output_aliases={0: 0},
            scratch_shapes=[pltpu.SemaphoreType.DMA((TAIL,))],
            compiler_params=pltpu.CompilerParams(vmem_limit_bytes=2**20),
            name="rest",
        )(written, pltpu.with_memory_space_constraint(tail, pltpu.VMEM))

    return jax.shard_map(
        local, mesh=mesh, in_specs=P(("rep", "dp")), out_specs=P("rep"), check_vma=False
    )
```

time: 324 us -> 314 us (0.969)
  Pallas kernels: 324 us -> 314 us
    pallas_call x1, Pallas kernels: 318 us -> 280 us  [local(): pl.pallas_call(functools.partial(ring_kernel, ranks), out_shape=pltpu.VME...]
    pallas_call x1 -> x3, Pallas kernels: 6.84 us -> 33.7 us  [the longest x1 26 us: local(): pl.pallas_call(functools.partial(tail_kernel, ranks), out_shape=pltpu.VME...]
where the time goes in v2:
time: 314 us
  Pallas kernels  314 us (100%)
    pallas_call x1, Pallas kernels, local(): pl.pallas_call(functools.partial(ring_kernel, ranks), out_shape=pltpu.VME...  280 us
    pallas_call x1, Pallas kernels, local(): pl.pallas_call(functools.partial(tail_kernel, ranks), out_shape=pltpu.VME...  26 us

profile of v2, /device:TPU:112, one launch (start us, length us, event | category | flops | bytes accessed | tf_op | source)
XLA Modules:
  0.0 314.0 jit_solution(2631016005451988873)
XLA Ops:
  0.0 280.3 %ring.1.sums = bf16[4,12,768,256]{3,2,1,0:T(8,128)(2,1)S(1)} custom-call(bf16[1,4,4096,768]{3,2,1,0:T(8,128)(2,1)} %a_hbm.1, bf16[1,4,4096,3072]{3,2,1,0:T(8,128)(2,1)} %g_hbm.1), custom_call_target="tpu_custom_call" | custom-call | tf_op jit(solution)/shard_map/ring/pallas_call | solution.py:283
  280.3 5.9 %write.1.written = bf16[4,768,3072]{2,1,0:T(8,128)(2,1)} custom-call(bf16[4,12,768,256]{3,2,1,0:T(8,128)(2,1)S(1)} %ring.1.sums), custom_call_target="tpu_custom_call" | custom-call | tf_op jit(solution)/shard_map/write/pallas_call | solution.py:306
  286.2 26.0 %tail.1 = bf16[8,768,256]{2,1,0:T(8,128)(2,1)S(1)} custom-call(bf16[4,12,768,256]{3,2,1,0:T(8,128)(2,1)S(1)} %ring.1.sums, bf16[4,768,3072]{2,1,0:T(8,128)(2,1)} %write.1.written), custom_call_target="tpu_custom_call" | custom-call | tf_op jit(solution)/shard_map/tail/pallas_call | solution.py:315
  312.2 1.7 rest.1

commit v3 on v2

--- a/solution.py
+++ b/solution.py
@@ -21,7 +21,7 @@
 
 
 def kept(units):
-    return units - TAIL + lax.rem(lax.axis_index("rep"), 2) * (TAIL - LAST)
+    return units - LAST - lax.rem(lax.axis_index("rep"), 2) * (TAIL - LAST)
 
 
 def greet(ranks):

time: 314 us -> 313 us (level)
    pallas_call x1, Pallas kernels: 26 us -> 11 us  [local(): pl.pallas_call(functools.partial(tail_kernel, ranks), out_shape=pltpu.VME...]
    pallas_call x1, Pallas kernels: 280 us -> 294 us  [local(): pl.pallas_call(functools.partial(ring_kernel, ranks), out_shape=pltpu.VME...]
where the time goes in v3:
time: 313 us
  Pallas kernels  312 us (100%)
    pallas_call x1, Pallas kernels, local(): pl.pallas_call(functools.partial(ring_kernel, ranks), out_shape=pltpu.VME...  294 us
    pallas_call x1, Pallas kernels, local(): pl.pallas_call(functools.partial(tail_kernel, ranks), out_shape=pltpu.VME...  11 us
    pallas_call x1, Pallas kernels, local(): pl.pallas_call(functools.partial(write_kernel, ranks), out_shape=whole, i...  6.61 us

profile of v3, /device:TPU:112, one launch (start us, length us, event | category | flops | bytes accessed | tf_op | source)
XLA Modules:
  0.0 312.5 jit_solution(207964807832008421)
XLA Ops:
  0.0 293.9 %ring.1.sums = bf16[4,12,768,256]{3,2,1,0:T(8,128)(2,1)S(1)} custom-call(bf16[1,4,4096,768]{3,2,1,0:T(8,128)(2,1)} %a_hbm.1, bf16[1,4,4096,3072]{3,2,1,0:T(8,128)(2,1)} %g_hbm.1), custom_call_target="tpu_custom_call" | custom-call | tf_op jit(solution)/shard_map/ring/pallas_call | solution.py:283
  293.9 6.6 %write.1.written = bf16[4,768,3072]{2,1,0:T(8,128)(2,1)} custom-call(bf16[4,12,768,256]{3,2,1,0:T(8,128)(2,1)S(1)} %ring.1.sums), custom_call_target="tpu_custom_call" | custom-call | tf_op jit(solution)/shard_map/write/pallas_call | solution.py:306
  300.5 11.0 %tail.1 = bf16[8,768,256]{2,1,0:T(8,128)(2,1)S(1)} custom-call(bf16[4,12,768,256]{3,2,1,0:T(8,128)(2,1)S(1)} %ring.1.sums, bf16[4,768,3072]{2,1,0:T(8,128)(2,1)} %write.1.written), custom_call_target="tpu_custom_call" | custom-call | tf_op jit(solution)/shard_map/tail/pallas_call | solution.py:315
  311.5 1.0 rest.1

commit v4 on v3

--- a/solution.py
+++ b/solution.py
@@ -10,6 +10,7 @@
 COLS = 256
 ROWS = 256
 FIRST = 128
+SHARES = 8
 TAIL, LAST = 8, 2
 SLOTS = 4
 
@@ -57,13 +58,16 @@
         columns = pl.ds(cuts[k], cuts[k + 1] - cuts[k])
         return pltpu.make_async_copy(a_hbm.at[0, 0, :, columns], a_v.at[0, :, columns], a0_sem.at[k])
 
+    def share(h):
+        return pl.ds(h * (tokens // SHARES), tokens // SHARES)
+
     def load_start(h):
-        half = pl.ds(h * (tokens // 2), tokens // 2)
-        copies = [(a_hbm.at[0, 0, half, pl.ds(0, FIRST)], a_v.at[0, half, pl.ds(0, FIRST)])]
+        some = share(h)
+        copies = [(a_hbm.at[0, 0, some, pl.ds(0, FIRST)], a_v.at[0, some, pl.ds(0, FIRST)])]
         for i in range(2):
             n, c = place_of(0, i)
             columns = pl.ds(pl.multiple_of(c * COLS, COLS), COLS)
-            copies.append((g_hbm.at[0, n, half, columns], g_v.at[half, pl.ds(i * COLS, COLS)]))
+            copies.append((g_hbm.at[0, n, some, columns], g_v.at[some, pl.ds(i * COLS, COLS)]))
         return [pltpu.make_async_copy(*copy, start_sem.at[h, k]) for k, copy in enumerate(copies)]
 
     def slot(i):
@@ -98,16 +102,16 @@
         def _():
             send(old // units, lax.rem(old, units)).wait_send()
 
-    for h in range(2):
+    for h in range(SHARES):
         for copy in load_start(h):
             copy.start()
 
     greet(ranks)
 
-    def term_of(n, half, top, bottom, columns):
+    def term_of(n, some, top, bottom, columns):
         return lax.dot_general(
-            a_v[n, half, top:bottom],
-            g_v[half, columns],
+            a_v[n, some, top:bottom],
+            g_v[some, columns],
             (((0,), (0,)), ((), ())),
             preferred_element_type=jnp.float32,
         )
@@ -117,14 +121,14 @@
         part = pl.ds(cuts[k], cuts[k + 1] - cuts[k])
         if k == 0:
             term = 0.0
-            for h in range(2):
+            for h in range(SHARES):
                 for copy in load_start(h):
                     copy.wait()
                 if h == 0:
                     for later in range(1, len(cuts) - 1):
                         load_a0(later).start()
                     load_g(2).start()
-                term += term_of(0, pl.ds(h * (tokens // 2), tokens // 2), 0, FIRST, both)
+                term += term_of(0, share(h), 0, FIRST, both)
         else:
             load_a0(k).wait()
             term = term_of(0, slice(None), cuts[k], cuts[k + 1], both)
@@ -138,11 +142,11 @@
     load_g(4).start()
     load_g(5).start()
 
-    def item(i, first):
+    def item(i, own):
         s, w = i // units, lax.rem(i, units)
         n = w // per_mat
 
-        if first:
+        if own:
 
             @pl.when(lax.rem(w, per_mat) == 0)
             def _():
@@ -153,14 +157,14 @@
                 load_a(n + 1).start()
 
         load_g(i).wait()
-        if not first:
+        if not own:
             arrived(s - 1, w)
             free(i)
         n, c = place_of(s, w)
         for top in range(0, rows, ROWS):
             part = pl.ds(top, ROWS)
             term = term_of(n, slice(None), top, top + ROWS, slot(i))
-            if not first:
+            if not own:
                 term += sums[n, c, part].astype(jnp.float32)
             sums[n, c, part] = term.astype(sums.dtype)
             send(s, w, (part,)).start()
@@ -291,7 +295,7 @@
                 pltpu.SemaphoreType.DMA((mats,)),
                 pltpu.SemaphoreType.DMA((1 + rows // ROWS,)),
                 pltpu.SemaphoreType.DMA((SLOTS,)),
-                pltpu.SemaphoreType.DMA((2, 3)),
+                pltpu.SemaphoreType.DMA((SHARES, 3)),
                 pltpu.SemaphoreType.DMA((phases, units)),
                 pltpu.SemaphoreType.DMA((phases, units)),
             ],

time: 313 us -> 312 us (level)
  no operation moved by 1% of the time
where the time goes in v4:
time: 312 us
  Pallas kernels  312 us (100%)
    pallas_call x1, Pallas kernels, local(): pl.pallas_call(functools.partial(ring_kernel, ranks), out_shape=pltpu.VME...  293 us
    pallas_call x1, Pallas kernels, local(): pl.pallas_call(functools.partial(tail_kernel, ranks), out_shape=pltpu.VME...  11.2 us
    pallas_call x1, Pallas kernels, local(): pl.pallas_call(functools.partial(write_kernel, ranks), out_shape=whole, i...  6.61 us

profile of v4, /device:TPU:112, one launch (start us, length us, event | category | flops | bytes accessed | tf_op | source)
XLA Modules:
  0.0 312.0 jit_solution(5407650599262597202)
XLA Ops:
  0.0 293.2 %ring.1.sums = bf16[4,12,768,256]{3,2,1,0:T(8,128)(2,1)S(1)} custom-call(bf16[1,4,4096,768]{3,2,1,0:T(8,128)(2,1)} %a_hbm.1, bf16[1,4,4096,3072]{3,2,1,0:T(8,128)(2,1)} %g_hbm.1), custom_call_target="tpu_custom_call" | custom-call | tf_op jit(solution)/shard_map/ring/pallas_call | solution.py:287
  293.2 6.6 %write.1.written = bf16[4,768,3072]{2,1,0:T(8,128)(2,1)} custom-call(bf16[4,12,768,256]{3,2,1,0:T(8,128)(2,1)S(1)} %ring.1.sums), custom_call_target="tpu_custom_call" | custom-call | tf_op jit(solution)/shard_map/write/pallas_call | solution.py:310
  299.8 11.2 %tail.1 = bf16[8,768,256]{2,1,0:T(8,128)(2,1)S(1)} custom-call(bf16[4,12,768,256]{3,2,1,0:T(8,128)(2,1)S(1)} %ring.1.sums, bf16[4,768,3072]{2,1,0:T(8,128)(2,1)} %write.1.written), custom_call_target="tpu_custom_call" | custom-call | tf_op jit(solution)/shard_map/tail/pallas_call | solution.py:319
  311.1 1.0 rest.1

commit v5 on v4

--- a/solution.py
+++ b/solution.py
@@ -19,6 +19,10 @@
     to_left = lax.rem(w, 2)
     b = lax.rem(me + 2 * ranks - s + to_left * (2 * s), ranks)
     return w // per_mat, lax.rem(w, per_mat) * ranks + b
+
+
+def columns_of(c):
+    return pl.ds(pl.multiple_of(c * COLS, COLS), COLS)
 
 
 def kept(units):
@@ -36,8 +40,8 @@
 
 
 def ring_kernel(ranks, a_hbm, g_hbm, sums, a_v, g_v, a_sem, a0_sem, g_sem, start_sem, send_sem, recv_sem):
-    mats, blocks, rows, _ = sums.shape
-    per_mat = blocks // ranks
+    mats, rows, width = sums.shape
+    per_mat = width // COLS // ranks
     units = mats * per_mat
     me = lax.axis_index("dp")
     right = lax.rem(me + 1, ranks)
@@ -78,9 +82,9 @@
         columns = pl.ds(pl.multiple_of(c * COLS, COLS), COLS)
         return pltpu.make_async_copy(g_hbm.at[0, n, :, columns], g_v.at[:, slot(i)], g_sem.at[lax.rem(i, SLOTS)])
 
-    def send(s, w, part=()):
+    def send(s, w, part=slice(None)):
         n, c = place_of(s, w)
-        block = sums.at[(n, c, *part)]
+        block = sums.at[n, part, columns_of(c)]
         to = right + lax.rem(w, 2) * (left - right)
         return pltpu.make_async_remote_copy(
             src_ref=block,
@@ -93,7 +97,8 @@
 
     def arrived(s, w):
         n, c = place_of(s + 1, w)
-        pltpu.make_async_copy(sums.at[n, c], sums.at[n, c], recv_sem.at[s, w]).wait()
+        block = sums.at[n, :, columns_of(c)]
+        pltpu.make_async_copy(block, block, recv_sem.at[s, w]).wait()
 
     def free(i):
         old = i - (ranks - 2) * units + 1
@@ -134,8 +139,8 @@
             term = term_of(0, slice(None), cuts[k], cuts[k + 1], both)
         for i in range(2):
             n, c = place_of(0, i)
-            sums[n, c, part] = term[:, i * COLS : (i + 1) * COLS].astype(sums.dtype)
-            send(0, i, (part,)).start()
+            sums[n, part, columns_of(c)] = term[:, i * COLS : (i + 1) * COLS].astype(sums.dtype)
+            send(0, i, part).start()
         if k == 0:
             load_a(1).start()
             load_g(3).start()
@@ -165,9 +170,9 @@
             part = pl.ds(top, ROWS)
             term = term_of(n, slice(None), top, top + ROWS, slot(i))
             if not own:
-                term += sums[n, c, part].astype(jnp.float32)
-            sums[n, c, part] = term.astype(sums.dtype)
-            send(s, w, (part,)).start()
+                term += sums[n, part, columns_of(c)].astype(jnp.float32)
+            sums[n, part, columns_of(c)] = term.astype(sums.dtype)
+            send(s, w, part).start()
 
         @pl.when(i + SLOTS < ranks * units)
         def _():
@@ -206,8 +211,8 @@
 
 def tail_kernel(ranks, sums, written, tail, send_sem, recv_sem):
     del written
-    mats, blocks = sums.shape[:2]
-    per_mat = blocks // ranks
+    mats, _, width = sums.shape
+    per_mat = width // COLS // ranks
     units = mats * per_mat
     me = lax.axis_index("dp")
     right = lax.rem(me + 1, ranks)
@@ -217,7 +222,7 @@
         n, c = place(ranks, per_mat, me, 2 * ranks - 3, w)
         t = w - (units - TAIL)
         return pltpu.make_async_remote_copy(
-            src_ref=sums.at[n, c],
+            src_ref=sums.at[n, :, columns_of(c)],
             dst_ref=tail.at[t],
             send_sem=send_sem.at[t],
             recv_sem=recv_sem.at[t],
@@ -238,22 +243,14 @@
     lax.fori_loop(kept(units), units, finish, 0)
 
 
-def write_kernel(ranks, sums, out, sem):
-    mats, blocks = sums.shape[:2]
-    per_mat = blocks // ranks
-    units = mats * per_mat
-    me = lax.axis_index("dp")
+def write_kernel(sums, out, sem):
+    mats, rows, _ = sums.shape
 
     def copies(act):
-        for w in range(units):
-            for s in range(ranks):
-                n, c = place(ranks, per_mat, me, s, w)
-                columns = pl.ds(pl.multiple_of(c * COLS, COLS), COLS)
-                copy = pltpu.make_async_copy(sums.at[n, c], out.at[n, :, columns], sem.at[w, s])
-                if s == ranks - 2 and w >= units - TAIL:
-                    pl.when(w < kept(units))(functools.partial(act, copy))
-                else:
-                    act(copy)
+        for n in range(mats):
+            for k in range(rows // FIRST):
+                part = pl.ds(k * FIRST, FIRST)
+                act(pltpu.make_async_copy(sums.at[n, part], out.at[n, part], sem.at[n, k]))
 
     copies(lambda copy: copy.start())
     copies(lambda copy: copy.wait())
@@ -286,7 +283,7 @@
         phases = 2 * ranks - 2
         sums = pl.pallas_call(
             functools.partial(ring_kernel, ranks),
-            out_shape=pltpu.VMEM((mats, blocks, rows, COLS), jnp.bfloat16),
+            out_shape=pltpu.VMEM((mats, rows, width), jnp.bfloat16),
             in_specs=[pl.BlockSpec(memory_space=pltpu.HBM)] * 2,
             out_specs=pl.BlockSpec(memory_space=pltpu.VMEM),
             scratch_shapes=[
@@ -308,11 +305,11 @@
         hbm, vmem = pl.BlockSpec(memory_space=pltpu.HBM), pl.BlockSpec(memory_space=pltpu.VMEM)
         whole = jax.ShapeDtypeStruct((mats, rows, width), jnp.bfloat16)
         written = pl.pallas_call(
-            functools.partial(write_kernel, ranks),
+            write_kernel,
             out_shape=whole,
             in_specs=[vmem],
             out_specs=hbm,
-            scratch_shapes=[pltpu.SemaphoreType.DMA((units, ranks))],
+            scratch_shapes=[pltpu.SemaphoreType.DMA((mats, rows // FIRST))],
             compiler_params=pltpu.CompilerParams(vmem_limit_bytes=2**20),
             name="write",
         )(sums)

time: 312 us -> 312 us (level)
  no operation moved by 1% of the time
where the time goes in v5:
time: 312 us
  Pallas kernels  312 us (100%)
    pallas_call x1, Pallas kernels, local(): pl.pallas_call(functools.partial(ring_kernel, ranks), out_shape=pltpu.VME...  292 us
    pallas_call x1, Pallas kernels, local(): pl.pallas_call(functools.partial(tail_kernel, ranks), out_shape=pltpu.VME...  12 us
    pallas_call x1, Pallas kernels, local(): pl.pallas_call(write_kernel, out_shape=whole, in_specs=[vmem], out_specs=...  6.66 us

profile of v5, /device:TPU:112, one launch (start us, length us, event | category | flops | bytes accessed | tf_op | source)
XLA Modules:
  0.0 312.0 jit_solution(3252789136406354120)
XLA Ops:
  0.0 292.4 %ring.1.sums = bf16[4,768,3072]{2,1,0:T(8,128)(2,1)S(1)} custom-call(bf16[1,4,4096,768]{3,2,1,0:T(8,128)(2,1)} %a_hbm.1, bf16[1,4,4096,3072]{3,2,1,0:T(8,128)(2,1)} %g_hbm.1), custom_call_target="tpu_custom_call" | custom-call | tf_op jit(solution)/shard_map/ring/pallas_call | solution.py:284
  292.4 6.7 %write.1.written = bf16[4,768,3072]{2,1,0:T(8,128)(2,1)} custom-call(bf16[4,768,3072]{2,1,0:T(8,128)(2,1)S(1)} %ring.1.sums), custom_call_target="tpu_custom_call" | custom-call | tf_op jit(solution)/shard_map/write/pallas_call | solution.py:307
  299.1 12.0 %tail.1 = bf16[8,768,256]{2,1,0:T(8,128)(2,1)S(1)} custom-call(bf16[4,768,3072]{2,1,0:T(8,128)(2,1)S(1)} %ring.1.sums, bf16[4,768,3072]{2,1,0:T(8,128)(2,1)} %write.1.written), custom_call_target="tpu_custom_call" | custom-call | tf_op jit(solution)/shard_map/tail/pallas_call | solution.py:316
  311.1 1.0 rest.1
